TPU v7x, 256 devices: a whole 4x4x8 slice. The times are simulated.
256 devices in a mesh: freq: 8 (over y, x_hi), rec: 32 (over x_lo, z, core).
Axes of the slice: x: 4 (x_hi: 2, x_lo: 2; x = x_hi * 2 + x_lo), y: 4, z: 8, core: 2. Of those that a mesh axis runs over, the one named last changes fastest.
Arguments:
- response: bfloat16 [128, 2, 1792, 1792], P('freq', None, 'rec'), may hold values from -1 to 1, as said below
- direct: float32 [1792, 32, 256], P('rec', 'freq'), may hold values from -6 to 6
- onset: int32 [1792, 32], P('rec', 'freq'), may hold values from 16 to 128
Outputs:
- upgoing: float32 [1792, 32, 256], P('rec', 'freq')
- coda: float32 [1792, 32, 256], P('rec', 'freq')
Inputs may be any that keep to these rules, and one draw needn't show every extreme that they name: response[k, c, r, s] = response[k, c, s, r] for every frequency and part (source-receiver reciprocity).
All inputs are finite; a program needn't handle non-finite values.
Results may differ from a plain program's by a relative error of at most 0.023.
Values may be sent and summed in bfloat16 or wider, within the bound.
A program may use at most 128 MiB of HBM per device.

v0:
```python
import math
import jax
import jax.numpy as jnp
from jax import lax
from jax.sharding import PartitionSpec as P

NF = 128
NT = 256
ITERS = 2


def spectral_tables(length, count):
    samples = jnp.arange(length, dtype=jnp.int32)
    frequency_bins = jnp.arange(1, count + 1, dtype=jnp.int32)
    phase = (samples[:, None] * frequency_bins[None, :] % length).astype(jnp.float32) * (
        2.0 * math.pi / length
    )
    cosine = jnp.cos(phase)
    sine = jnp.sin(phase)
    forward = jnp.stack([cosine, -sine], axis=1)
    inverse = jnp.stack([cosine.T, -sine.T], axis=0) * (2.0 / length)
    return (forward, inverse)


def make_window(onset, length):
    samples = jnp.arange(length, dtype=jnp.int32)
    folded = jnp.minimum(samples, length - samples)
    return (folded[None, None, :] < onset[:, :, None]).astype(jnp.float32)


def to_spectrum(field, forward):
    packed = jnp.einsum("svt,tck->kcvs", field, forward)
    return packed.astype(jnp.bfloat16)


def to_time(spectra, inverse):
    return jnp.einsum("kcvs,ckt->svt", spectra.astype(jnp.float32), inverse)


def complex_apply(block, spectra, conj_sign):
    parts = jnp.einsum("fcrs,fdvs->cdfvr", block, spectra, preferred_element_type=jnp.float32)
    real_out = parts[0, 0] - conj_sign * parts[1, 1]
    imag_out = parts[0, 1] + conj_sign * parts[1, 0]
    return jnp.stack([real_out, imag_out], axis=1)


def body(response, direct, onset):
    forward, inverse = spectral_tables(NT, NF)
    window = make_window(onset, NT)
    coda = jnp.zeros_like(direct)
    upgoing = coda
    for iteration in range(ITERS):
        downgoing = direct + coda
        sources = lax.all_to_all(
            to_spectrum(downgoing, forward), "freq", split_axis=0, concat_axis=2, tiled=True
        )
        gathered = lax.all_gather(sources, "rec", axis=3, tiled=True)
        reflected = complex_apply(response, gathered, 1.0)
        reflected_time = lax.all_to_all(
            reflected.astype(jnp.bfloat16), "freq", split_axis=2, concat_axis=0, tiled=True
        )
        upgoing = window * to_time(reflected_time, inverse)
        spectra_up = lax.all_to_all(
            to_spectrum(upgoing, forward), "freq", split_axis=0, concat_axis=2, tiled=True
        )
        receivers = lax.all_gather(spectra_up, "rec", axis=3, tiled=True)
        returned = complex_apply(response, receivers, -1.0)
        returned_time = lax.all_to_all(
            returned.astype(jnp.bfloat16), "freq", split_axis=2, concat_axis=0, tiled=True
        )
        coda = window * to_time(returned_time, inverse)
    return (upgoing, coda)


def solution(mesh):
    placed = (P("freq", None, "rec", None), P("rec", "freq", None), P("rec", "freq"))
    return jax.shard_map(
        body,
        mesh=mesh,
        in_specs=placed,
        out_specs=(P("rec", "freq", None), P("rec", "freq", None)),
        check_vma=False,
    )
```

profile of v0, /device:TPU:96, one launch (start us, length us, event | category | flops | bytes accessed | tf_op | source)
XLA Modules:
  0.0 545.7 jit_solution(14085154062390279766)
XLA Ops:
  7.2 0.5 fusion.96
  7.8 1.1 fusion.39
  9.5 14.9 %all_to_all.144 = bf16[8,2,3584]{2,1,0:T(2,128)(2,1)S(1)} all-to-all(bf16[8,2,3584]{2,1,0:T(2,128)(2,1)S(1)} %reshape.396), channel_id=1, replica_groups=mesh['freq'=8,'rec'=32] {'freq'}, dimensions={0} | all-to-all | bytes 229376 | tf_op jit(solution)/shard_map/all_to_all | solution.py:54
  24.9 1.5 copy.89
  26.4 0.6 fusion.97
  27.0 87.4 %all-gather.5.cloned.1.call-done = bf16[16,2,32,1792]{2,0,1,3:T(8,128)(2,1)} async-done(((bf16[16,2,32,56]{2,0,1,3:T(8,128)(2,1)}), bf16[16,2,32,1792]{2,0,1,3:T(8,128)(2,1)}) %all-gather.5.cloned.1.call-update) | async-done | bytes 3670032 | tf_op jit(solution)/shard_map/all_gather | solution.py:57
  114.4 15.0 %fusion.17 = f32[2,2,16,32,56]{4,3,0,1,2:T(8,128)S(1)} fusion(bf16[16,2,56,1792]{3,2,1,0:T(8,128)(2,1)} %param.3, bf16[16,2,32,1792,1]{2,0,1,3,4:T(8,128)(2,1)} %bitcast.271), kind=kOutput, calls=%fused_computation.13 | convolution fusion | flops 411041792 | bytes 10551296 | tf_op jit(solution)/shard_map/fcrs,fdvs->cdfvr/dot_general | solution.py:41
  129.7 1.1 reshape.398
  130.8 6.7 %all-to-all-start.1 = ((bf16[8,2,3584]{2,1,0:T(2,128)(2,1)}), bf16[8,2,3584]{2,1,0:T(2,128)(2,1)S(1)}, u32[]{:S(2)}, u32[]{:S(2)}) async-start(bf16[8,2,3584]{2,1,0:T(2,128)(2,1)} %reshape.398), calls=%async_computation.1 | async-start | bytes 229376 | tf_op jit(solution)/shard_map/all_to_all | solution.py:59
  137.6 8.1 %all-to-all-done.1 = bf16[8,2,3584]{2,1,0:T(2,128)(2,1)S(1)} async-done(((bf16[8,2,3584]{2,1,0:T(2,128)(2,1)}), bf16[8,2,3584]{2,1,0:T(2,128)(2,1)S(1)}, u32[]{:S(2)}, u32[]{:S(2)}) %all-to-all-start.1) | async-done | bytes 114720 | tf_op jit(solution)/shard_map/all_to_all | solution.py:59
  145.6 0.4 reshape.399
  147.1 10.5 %all_to_all.145 = bf16[8,2,3584]{2,1,0:T(2,128)(2,1)S(1)} all-to-all(bf16[8,2,3584]{2,1,0:T(2,128)(2,1)S(1)} %reshape.400), channel_id=1, replica_groups=mesh['freq'=8,'rec'=32] {'freq'}, dimensions={0} | all-to-all | bytes 229376 | tf_op jit(solution)/shard_map/all_to_all | solution.py:63
  158.2 1.5 copy.99
  159.9 85.8 %all-gather.7.cloned.1.call-done = bf16[16,2,32,1792]{2,0,1,3:T(8,128)(2,1)} async-done(((bf16[16,2,32,56]{2,0,1,3:T(8,128)(2,1)}), bf16[16,2,32,1792]{2,0,1,3:T(8,128)(2,1)}) %all-gather.7.cloned.1.call-update) | async-done | bytes 3670032 | tf_op jit(solution)/shard_map/all_gather | solution.py:66
  245.6 15.1 %fusion.22 = f32[2,2,16,32,56]{4,3,0,1,2:T(8,128)S(1)} fusion(bf16[16,2,56,1792]{3,2,1,0:T(8,128)(2,1)} %param.3, bf16[16,2,32,1792,1]{2,0,1,3,4:T(8,128)(2,1)} %bitcast.272), kind=kOutput, calls=%fused_computation.14 | convolution fusion | flops 411041792 | bytes 10551296 | tf_op jit(solution)/shard_map/fcrs,fdvs->cdfvr/dot_general | solution.py:41
  261.4 14.6 %all_to_all.146 = bf16[8,2,3584]{2,1,0:T(2,128)(2,1)S(1)} all-to-all(bf16[8,2,3584]{2,1,0:T(2,128)(2,1)S(1)} %reshape.402), channel_id=1, replica_groups=mesh['freq'=8,'rec'=32] {'freq'}, dimensions={0} | all-to-all | bytes 229376 | tf_op jit(solution)/shard_map/all_to_all | solution.py:68
  277.5 10.5 %all_to_all.147 = bf16[8,2,3584]{2,1,0:T(2,128)(2,1)S(1)} all-to-all(bf16[8,2,3584]{2,1,0:T(2,128)(2,1)S(1)} %reshape.404), channel_id=1, replica_groups=mesh['freq'=8,'rec'=32] {'freq'}, dimensions={0} | all-to-all | bytes 229376 | tf_op jit(solution)/shard_map/all_to_all | solution.py:54
  288.6 1.5 copy.111
  290.3 85.7 %all-gather.9.cloned.1.call-done = bf16[16,2,32,1792]{2,0,1,3:T(8,128)(2,1)} async-done(((bf16[16,2,32,56]{2,0,1,3:T(8,128)(2,1)}), bf16[16,2,32,1792]{2,0,1,3:T(8,128)(2,1)}) %all-gather.9.cloned.1.call-update) | async-done | bytes 3670032 | tf_op jit(solution)/shard_map/all_gather | solution.py:57
  376.0 15.0 %fusion.27 = f32[2,2,16,32,56]{4,3,0,1,2:T(8,128)S(1)} fusion(bf16[16,2,56,1792]{3,2,1,0:T(8,128)(2,1)} %param.3, bf16[16,2,32,1792,1]{2,0,1,3,4:T(8,128)(2,1)} %bitcast.273), kind=kOutput, calls=%fused_computation.15 | convolution fusion | flops 411041792 | bytes 10551296 | tf_op jit(solution)/shard_map/fcrs,fdvs->cdfvr/dot_general | solution.py:41
  391.8 14.6 %all_to_all.148 = bf16[8,2,3584]{2,1,0:T(2,128)(2,1)S(1)} all-to-all(bf16[8,2,3584]{2,1,0:T(2,128)(2,1)S(1)} %reshape.406), channel_id=1, replica_groups=mesh['freq'=8,'rec'=32] {'freq'}, dimensions={0} | all-to-all | bytes 229376 | tf_op jit(solution)/shard_map/all_to_all | solution.py:59
  407.9 10.5 %all_to_all.149 = bf16[8,2,3584]{2,1,0:T(2,128)(2,1)S(1)} all-to-all(bf16[8,2,3584]{2,1,0:T(2,128)(2,1)S(1)} %reshape.408), channel_id=1, replica_groups=mesh['freq'=8,'rec'=32] {'freq'}, dimensions={0} | all-to-all | bytes 229376 | tf_op jit(solution)/shard_map/all_to_all | solution.py:63
  418.5 0.4 reshape.409
  419.0 1.5 copy.121
  420.5 86.0 %all-gather.11.cloned.1.call-done = bf16[16,2,32,1792]{2,0,1,3:T(8,128)(2,1)} async-done(((bf16[16,2,32,56]{2,0,1,3:T(8,128)(2,1)}), bf16[16,2,32,1792]{2,0,1,3:T(8,128)(2,1)}) %all-gather.11.cloned.1.call-update) | async-done | bytes 3670032 | tf_op jit(solution)/shard_map/all_gather | solution.py:66
  506.5 15.0 %fusion.12 = f32[2,2,16,32,56]{4,3,2,1,0:T(8,128)S(1)} fusion(bf16[16,2,32,1792,1]{2,0,1,3,4:T(8,128)(2,1)} %bitcast.274, bf16[16,2,56,1792]{3,2,1,0:T(8,128)(2,1)} %param.3), kind=kOutput, calls=%fused_computation.12 | convolution fusion | flops 411041792 | bytes 10551296 | tf_op jit(solution)/shard_map/fcrs,fdvs->cdfvr/dot_general | solution.py:41
  521.8 1.1 reshape.410
  522.8 6.7 %all-to-all-start.7 = ((bf16[8,2,3584]{2,1,0:T(2,128)(2,1)}), bf16[8,2,3584]{2,1,0:T(2,128)(2,1)S(1)}, u32[]{:S(2)}, u32[]{:S(2)}) async-start(bf16[8,2,3584]{2,1,0:T(2,128)(2,1)} %reshape.410), calls=%async_computation.7 | async-start | bytes 229376 | tf_op jit(solution)/shard_map/all_to_all | solution.py:68
  529.5 0.8 copy.127
  530.3 7.4 %all-to-all-done.7 = bf16[8,2,3584]{2,1,0:T(2,128)(2,1)S(1)} async-done(((bf16[8,2,3584]{2,1,0:T(2,128)(2,1)}), bf16[8,2,3584]{2,1,0:T(2,128)(2,1)S(1)}, u32[]{:S(2)}, u32[]{:S(2)}) %all-to-all-start.7) | async-done | bytes 114720 | tf_op jit(solution)/shard_map/all_to_all | solution.py:68
  537.7 0.4 reshape.411
  538.4 0.8 copy.128
  (61 shorter events, 8.8 us)
Async XLA Ops:
  7.2 107.3 %all-gather.5.cloned.1.call-start = ((), (), s32[]{:S(2)}) async-start(), calls=%async_computation.8 | async-start | bytes 15138816 | tf_op jit(solution)/shard_map/all_gather | solution.py:57
  114.4 31.7 %copy-start.1 = (s32[56,4]{0,1:T(4,128)S(1)}, s32[56,4]{0,1:T(4,128)}, u32[]{:S(2)}) copy-start(s32[56,4]{0,1:T(4,128)} %param.5) | copy-start | bytes 2692
  130.8 14.8 %all-to-all-start.1 = ((bf16[8,2,3584]{2,1,0:T(2,128)(2,1)}), bf16[8,2,3584]{2,1,0:T(2,128)(2,1)S(1)}, u32[]{:S(2)}, u32[]{:S(2)}) async-start(bf16[8,2,3584]{2,1,0:T(2,128)(2,1)} %reshape.398), calls=%async_computation.1 | async-start | bytes 229376 | tf_op jit(solution)/shard_map/all_to_all | solution.py:59
  137.5 108.1 %all-gather.7.cloned.1.call-start = ((), (), s32[]{:S(2)}) async-start(), calls=%async_computation.9 | async-start | bytes 15138816 | tf_op jit(solution)/shard_map/all_gather | solution.py:66
  159.6 216.4 %all-gather.9.cloned.1.call-start = ((), (), s32[]{:S(2)}) async-start(), calls=%async_computation.10 | async-start | bytes 15138816 | tf_op jit(solution)/shard_map/all_gather | solution.py:57
  245.6 30.9 %copy-start = (f32[56,4,256]{2,1,0:T(4,128)S(1)}, f32[56,4,256]{2,1,0:T(4,128)}, u32[]{:S(2)}) copy-start(f32[56,4,256]{2,1,0:T(4,128)} %param.4) | copy-start | bytes 688132
  290.1 216.4 %all-gather.11.cloned.1.call-start = ((), (), s32[]{:S(2)}) async-start(), calls=%async_computation.11 | async-start | bytes 15138816 | tf_op jit(solution)/shard_map/all_gather | solution.py:66
  522.8 14.8 %all-to-all-start.7 = ((bf16[8,2,3584]{2,1,0:T(2,128)(2,1)}), bf16[8,2,3584]{2,1,0:T(2,128)(2,1)S(1)}, u32[]{:S(2)}, u32[]{:S(2)}) async-start(bf16[8,2,3584]{2,1,0:T(2,128)(2,1)} %reshape.410), calls=%async_computation.7 | async-start | bytes 229376 | tf_op jit(solution)/shard_map/all_to_all | solution.py:68
Sparse Core Ops, SparseCore 0:
  26.5 87.8 all-gather.4
  159.8 85.8 all-gather.6
  290.2 85.8 all-gather.8
  420.6 85.8 all-gather.10
where the time goes:
time: 546 us
  waiting for transfers between devices  360 us (66%)
  blocking collectives  75.7 us (14%)
  matrix products  62.6 us (11%)
  local copies, waits for them, and re-layouts  17 us (3%)
  between operations  14.2 us (3%)
  starting transfers between devices  14 us (3%)
    all_gather x2, waiting for transfers between devices, body(): gathered = lax.all_gather(sources, 'rec', axis=3, tiled=True)  173 us
    all_gather x2, waiting for transfers between devices, body(): receivers = lax.all_gather(spectra_up, 'rec', axis=3, tiled=True)  172 us
    dot_general x4, matrix products, complex_apply(): jnp.einsum('fcrs,fdvs->cdfvr', block, spectra, preferred_element_type=jnp...  60.1 us
    all_to_all x2, blocking collectives, body(): lax.all_to_all(to_spectrum(downgoing, forward), 'freq', split_axis=0, con...  25.4 us
    all_to_all x2, blocking collectives, body(): lax.all_to_all(to_spectrum(upgoing, forward), 'freq', split_axis=0, conca...  21.1 us
    all_to_all x1, blocking collectives, body(): lax.all_to_all(reflected.astype(jnp.bfloat16), 'freq', split_axis=2, conc...  14.6 us
    all_to_all x1, blocking collectives, body(): lax.all_to_all(returned.astype(jnp.bfloat16), 'freq', split_axis=2, conca...  14.6 us
  transfers between devices with their start and end apart: 6, of which 6 were waited for; matrix products, arithmetic and copies ran while one was open for 0% of the time, Pallas kernels for 0%

commit v1 on v0

--- a/solution.py
+++ b/solution.py
@@ -51,9 +51,11 @@
     upgoing = coda
     for iteration in range(ITERS):
         downgoing = direct + coda
-        sources = lax.all_to_all(
-            to_spectrum(downgoing, forward), "freq", split_axis=0, concat_axis=2, tiled=True
-        )
+        part = to_spectrum(downgoing, forward)
+        size = lax.axis_size("freq")
+        blocks = jnp.stack(jnp.split(part, size, axis=0), axis=0)
+        blocks = lax.all_to_all(blocks, "freq", split_axis=0, concat_axis=0)
+        sources = jnp.concatenate(blocks, axis=2)
         gathered = lax.all_gather(sources, "rec", axis=3, tiled=True)
         reflected = complex_apply(response, gathered, 1.0)
         reflected_time = lax.all_to_all(

time: 546 us -> 557 us (1.020); the launches traced: 546 us -> 549 us
  no operation moved by 1% of the time
where the time goes in v1:
time: 557 us; the launch traced here: 549 us
  waiting for transfers between devices  361 us (65%)
  blocking collectives  76.4 us (14%)
  matrix products  62.6 us (11%)
  local copies, waits for them, and re-layouts  18.9 us (3%)
  between operations  14.5 us (3%)
  starting transfers between devices  13.7 us (2%)
    all_gather x2, waiting for transfers between devices, body(): gathered = lax.all_gather(sources, 'rec', axis=3, tiled=True)  173 us
    all_gather x2, waiting for transfers between devices, body(): receivers = lax.all_gather(spectra_up, 'rec', axis=3, tiled=True)  172 us
    dot_general x4, matrix products, complex_apply(): jnp.einsum('fcrs,fdvs->cdfvr', block, spectra, preferred_element_type=jnp...  60.1 us
    all_to_all x2, blocking collectives, body(): blocks = lax.all_to_all(blocks, 'freq', split_axis=0, concat_axis=0)  25.4 us
    all_to_all x2, blocking collectives, body(): lax.all_to_all(to_spectrum(upgoing, forward), 'freq', split_axis=0, conca...  21.7 us
    all_to_all x1, blocking collectives, body(): lax.all_to_all(returned.astype(jnp.bfloat16), 'freq', split_axis=2, conca...  14.6 us
    all_to_all x1, blocking collectives, body(): lax.all_to_all(reflected.astype(jnp.bfloat16), 'freq', split_axis=2, conc...  14.6 us
  transfers between devices with their start and end apart: 6, of which 6 were waited for; matrix products, arithmetic and copies ran while one was open for 0% of the time, Pallas kernels for 0%

profile of v1, /device:TPU:96, one launch (start us, length us, event | category | flops | bytes accessed | tf_op | source)
XLA Modules:
  0.0 548.6 jit_solution(10758730276400449760)
XLA Ops:
  7.2 0.5 fusion.96
  7.8 1.1 fusion.39
  10.6 14.9 %all_to_all.118 = bf16[8,2,3584]{2,1,0:T(2,128)(2,1)S(1)} all-to-all(bf16[8,2,3584]{2,1,0:T(2,128)(2,1)S(1)} %reshape.412), channel_id=1, replica_groups=mesh['freq'=8,'rec'=32] {'freq'}, dimensions={0} | all-to-all | bytes 229376 | tf_op jit(solution)/shard_map/all_to_all | solution.py:57
  25.4 0.4 reshape.413
  25.9 1.5 copy.109
  27.4 0.6 fusion.97
  28.0 87.4 %all-gather.5.cloned.1.call-done = bf16[16,2,32,1792]{2,0,1,3:T(8,128)(2,1)} async-done(((bf16[16,2,32,56]{2,0,1,3:T(8,128)(2,1)}), bf16[16,2,32,1792]{2,0,1,3:T(8,128)(2,1)}) %all-gather.5.cloned.1.call-update) | async-done | bytes 3670032 | tf_op jit(solution)/shard_map/all_gather | solution.py:59
  115.4 15.0 %fusion.17 = f32[2,2,16,32,56]{4,3,0,1,2:T(8,128)S(1)} fusion(bf16[16,2,56,1792]{3,2,1,0:T(8,128)(2,1)} %param.3, bf16[16,2,32,1792,1]{2,0,1,3,4:T(8,128)(2,1)} %bitcast.307), kind=kOutput, calls=%fused_computation.13 | convolution fusion | flops 411041792 | bytes 10551296 | tf_op jit(solution)/shard_map/fcrs,fdvs->cdfvr/dot_general | solution.py:41
  130.8 1.1 reshape.414
  131.8 6.7 %all-to-all-start.1 = ((bf16[8,2,3584]{2,1,0:T(2,128)(2,1)}), bf16[8,2,3584]{2,1,0:T(2,128)(2,1)S(1)}, u32[]{:S(2)}, u32[]{:S(2)}) async-start(bf16[8,2,3584]{2,1,0:T(2,128)(2,1)} %reshape.414), calls=%async_computation.1 | async-start | bytes 229376 | tf_op jit(solution)/shard_map/all_to_all | solution.py:61
  138.6 8.1 %all-to-all-done.1 = bf16[8,2,3584]{2,1,0:T(2,128)(2,1)S(1)} async-done(((bf16[8,2,3584]{2,1,0:T(2,128)(2,1)}), bf16[8,2,3584]{2,1,0:T(2,128)(2,1)S(1)}, u32[]{:S(2)}, u32[]{:S(2)}) %all-to-all-start.1) | async-done | bytes 114720 | tf_op jit(solution)/shard_map/all_to_all | solution.py:61
  146.7 0.4 reshape.415
  148.1 11.0 %all_to_all.119 = bf16[8,2,3584]{2,1,0:T(2,128)(2,1)S(1)} all-to-all(bf16[8,2,3584]{2,1,0:T(2,128)(2,1)S(1)} %reshape.416), channel_id=1, replica_groups=mesh['freq'=8,'rec'=32] {'freq'}, dimensions={0} | all-to-all | bytes 229376 | tf_op jit(solution)/shard_map/all_to_all | solution.py:65
  159.6 1.5 copy.119
  161.2 85.9 %all-gather.7.cloned.1.call-done = bf16[16,2,32,1792]{2,0,1,3:T(8,128)(2,1)} async-done(((bf16[16,2,32,56]{2,0,1,3:T(8,128)(2,1)}), bf16[16,2,32,1792]{2,0,1,3:T(8,128)(2,1)}) %all-gather.7.cloned.1.call-update) | async-done | bytes 3670032 | tf_op jit(solution)/shard_map/all_gather | solution.py:68
  247.1 15.1 %fusion.22 = f32[2,2,16,32,56]{4,3,0,1,2:T(8,128)S(1)} fusion(bf16[16,2,56,1792]{3,2,1,0:T(8,128)(2,1)} %param.3, bf16[16,2,32,1792,1]{2,0,1,3,4:T(8,128)(2,1)} %bitcast.308), kind=kOutput, calls=%fused_computation.14 | convolution fusion | flops 411041792 | bytes 10551296 | tf_op jit(solution)/shard_map/fcrs,fdvs->cdfvr/dot_general | solution.py:41
  262.9 14.6 %all_to_all.120 = bf16[8,2,3584]{2,1,0:T(2,128)(2,1)S(1)} all-to-all(bf16[8,2,3584]{2,1,0:T(2,128)(2,1)S(1)} %reshape.418), channel_id=1, replica_groups=mesh['freq'=8,'rec'=32] {'freq'}, dimensions={0} | all-to-all | bytes 229376 | tf_op jit(solution)/shard_map/all_to_all | solution.py:70
  280.0 10.5 %all_to_all.121 = bf16[8,2,3584]{2,1,0:T(2,128)(2,1)S(1)} all-to-all(bf16[8,2,3584]{2,1,0:T(2,128)(2,1)S(1)} %reshape.420), channel_id=1, replica_groups=mesh['freq'=8,'rec'=32] {'freq'}, dimensions={0} | all-to-all | bytes 229376 | tf_op jit(solution)/shard_map/all_to_all | solution.py:57
  291.0 1.5 copy.137
  292.7 85.8 %all-gather.9.cloned.1.call-done = bf16[16,2,32,1792]{2,0,1,3:T(8,128)(2,1)} async-done(((bf16[16,2,32,56]{2,0,1,3:T(8,128)(2,1)}), bf16[16,2,32,1792]{2,0,1,3:T(8,128)(2,1)}) %all-gather.9.cloned.1.call-update) | async-done | bytes 3670032 | tf_op jit(solution)/shard_map/all_gather | solution.py:59
  378.5 15.0 %fusion.27 = f32[2,2,16,32,56]{4,3,0,1,2:T(8,128)S(1)} fusion(bf16[16,2,56,1792]{3,2,1,0:T(8,128)(2,1)} %param.3, bf16[16,2,32,1792,1]{2,0,1,3,4:T(8,128)(2,1)} %bitcast.309), kind=kOutput, calls=%fused_computation.15 | convolution fusion | flops 411041792 | bytes 10551296 | tf_op jit(solution)/shard_map/fcrs,fdvs->cdfvr/dot_general | solution.py:41
  394.2 14.6 %all_to_all.122 = bf16[8,2,3584]{2,1,0:T(2,128)(2,1)S(1)} all-to-all(bf16[8,2,3584]{2,1,0:T(2,128)(2,1)S(1)} %reshape.422), channel_id=1, replica_groups=mesh['freq'=8,'rec'=32] {'freq'}, dimensions={0} | all-to-all | bytes 229376 | tf_op jit(solution)/shard_map/all_to_all | solution.py:61
  410.4 10.7 %all_to_all.123 = bf16[8,2,3584]{2,1,0:T(2,128)(2,1)S(1)} all-to-all(bf16[8,2,3584]{2,1,0:T(2,128)(2,1)S(1)} %reshape.424), channel_id=1, replica_groups=mesh['freq'=8,'rec'=32] {'freq'}, dimensions={0} | all-to-all | bytes 229376 | tf_op jit(solution)/shard_map/all_to_all | solution.py:65
  421.1 0.4 reshape.425
  421.6 1.5 copy.147
  423.1 86.0 %all-gather.11.cloned.1.call-done = bf16[16,2,32,1792]{2,0,1,3:T(8,128)(2,1)} async-done(((bf16[16,2,32,56]{2,0,1,3:T(8,128)(2,1)}), bf16[16,2,32,1792]{2,0,1,3:T(8,128)(2,1)}) %all-gather.11.cloned.1.call-update) | async-done | bytes 3670032 | tf_op jit(solution)/shard_map/all_gather | solution.py:68
  509.1 15.0 %fusion.12 = f32[2,2,16,32,56]{4,3,2,1,0:T(8,128)S(1)} fusion(bf16[16,2,32,1792,1]{2,0,1,3,4:T(8,128)(2,1)} %bitcast.310, bf16[16,2,56,1792]{3,2,1,0:T(8,128)(2,1)} %param.3), kind=kOutput, calls=%fused_computation.12 | convolution fusion | flops 411041792 | bytes 10551296 | tf_op jit(solution)/shard_map/fcrs,fdvs->cdfvr/dot_general | solution.py:41
  524.4 1.1 reshape.426
  525.5 6.7 %all-to-all-start.7 = ((bf16[8,2,3584]{2,1,0:T(2,128)(2,1)}), bf16[8,2,3584]{2,1,0:T(2,128)(2,1)S(1)}, u32[]{:S(2)}, u32[]{:S(2)}) async-start(bf16[8,2,3584]{2,1,0:T(2,128)(2,1)} %reshape.426), calls=%async_computation.7 | async-start | bytes 229376 | tf_op jit(solution)/shard_map/all_to_all | solution.py:70
  532.2 0.8 copy.153
  533.0 7.4 %all-to-all-done.7 = bf16[8,2,3584]{2,1,0:T(2,128)(2,1)S(1)} async-done(((bf16[8,2,3584]{2,1,0:T(2,128)(2,1)}), bf16[8,2,3584]{2,1,0:T(2,128)(2,1)S(1)}, u32[]{:S(2)}, u32[]{:S(2)}) %all-to-all-start.7) | async-done | bytes 114720 | tf_op jit(solution)/shard_map/all_to_all | solution.py:70
  541.0 0.8 copy.154
  (91 shorter events, 10.5 us)
Async XLA Ops:
  7.2 108.3 %all-gather.5.cloned.1.call-start = ((), (), s32[]{:S(2)}) async-start(), calls=%async_computation.8 | async-start | bytes 15138816 | tf_op jit(solution)/shard_map/all_gather | solution.py:59
  115.4 31.7 %copy-start.1 = (s32[56,4]{0,1:T(4,128)S(1)}, s32[56,4]{0,1:T(4,128)}, u32[]{:S(2)}) copy-start(s32[56,4]{0,1:T(4,128)} %param.5) | copy-start | bytes 2692
  131.8 14.8 %all-to-all-start.1 = ((bf16[8,2,3584]{2,1,0:T(2,128)(2,1)}), bf16[8,2,3584]{2,1,0:T(2,128)(2,1)S(1)}, u32[]{:S(2)}, u32[]{:S(2)}) async-start(bf16[8,2,3584]{2,1,0:T(2,128)(2,1)} %reshape.414), calls=%async_computation.1 | async-start | bytes 229376 | tf_op jit(solution)/shard_map/all_to_all | solution.py:61
  138.5 108.6 %all-gather.7.cloned.1.call-start = ((), (), s32[]{:S(2)}) async-start(), calls=%async_computation.9 | async-start | bytes 15138816 | tf_op jit(solution)/shard_map/all_gather | solution.py:68
  161.1 217.4 %all-gather.9.cloned.1.call-start = ((), (), s32[]{:S(2)}) async-start(), calls=%async_computation.10 | async-start | bytes 15138816 | tf_op jit(solution)/shard_map/all_gather | solution.py:59
  247.1 30.9 %copy-start = (f32[56,4,256]{2,1,0:T(4,128)S(1)}, f32[56,4,256]{2,1,0:T(4,128)}, u32[]{:S(2)}) copy-start(f32[56,4,256]{2,1,0:T(4,128)} %param.4) | copy-start | bytes 688132
  292.5 216.6 %all-gather.11.cloned.1.call-start = ((), (), s32[]{:S(2)}) async-start(), calls=%async_computation.11 | async-start | bytes 15138816 | tf_op jit(solution)/shard_map/all_gather | solution.py:68
  525.5 14.8 %all-to-all-start.7 = ((bf16[8,2,3584]{2,1,0:T(2,128)(2,1)}), bf16[8,2,3584]{2,1,0:T(2,128)(2,1)S(1)}, u32[]{:S(2)}, u32[]{:S(2)}) async-start(bf16[8,2,3584]{2,1,0:T(2,128)(2,1)} %reshape.426), calls=%async_computation.7 | async-start | bytes 229376 | tf_op jit(solution)/shard_map/all_to_all | solution.py:70
Sparse Core Ops, SparseCore 0:
  27.5 87.8 all-gather.4
  161.2 85.8 all-gather.6
  292.6 85.8 all-gather.8
  423.2 85.8 all-gather.10
